TPU v7x, 32 devices: a whole 2x2x4 slice. The times are simulated.
32 devices in a mesh: dp: 8 (over z, x), tensor: 4 (over y, core).
Axes of the slice: x: 2, y: 2, z: 4, core: 2. Of those that a mesh axis runs over, the one named last changes fastest.
Arguments:
- residual: bfloat16 [2, 512, 5120], P(None, 'dp'), may hold values from -6 to 6
- context: bfloat16 [2, 512, 1536], P(None, 'dp', 'tensor'), may hold values from -6 to 6
- w_out: bfloat16 [1536, 5120], P('tensor'), may hold values from -0.15625 to 0.15625
- gain: float32 [5120], replicated, may hold values from 0.1 to 1.9
- cotangent: bfloat16 [2, 512, 5120], P(None, 'dp'), may hold values from -6 to 6
- slot_rows: int32 [4, 32], P('tensor'), may hold values from 0 to 383, as said below
Outputs:
- grad_slots: float32 [4, 5120, 32], P('tensor', 'dp')
- ctx_grad: bfloat16 [2, 512, 1536], P(None, 'dp', 'tensor')
- resid_grad: bfloat16 [2, 512, 5120], P(None, 'dp')
Inputs may be any that keep to these rules, and one draw needn't show every extreme that they name: Each row of slot_rows holds 32 different numbers.
All inputs are finite; a program needn't handle non-finite values.
Results may differ from a plain program's by a relative error of at most 0.006.
Values may be sent and summed in bfloat16 or wider, within the bound.
A program may use at most 64 MiB of HBM per device.

v0:
```python
import jax
import jax.numpy as jnp
from jax import lax
from jax.sharding import PartitionSpec as P


def norm_backward(res_rows, summed, gain, cot_rows):
    hidden = res_rows.astype(jnp.float32) + summed
    center = hidden - jnp.mean(hidden, axis=-1, keepdims=True)
    inverse = lax.rsqrt(jnp.mean(center * center, axis=-1, keepdims=True) + 1e-05)
    normed = center * inverse
    upstream = cot_rows.astype(jnp.float32) * gain
    result = inverse * (
        upstream
        - jnp.mean(upstream, axis=-1, keepdims=True)
        - normed * jnp.mean(upstream * normed, axis=-1, keepdims=True)
    )
    return result.astype(jnp.bfloat16)


def weight_term(grad_rows, columns):
    return lax.dot_general(
        grad_rows, columns, (((0,), (0,)), ((), ())), preferred_element_type=jnp.float32
    )


def body(residual, context, w_out, gain, cotangent, slot_rows):
    micro_count = residual.shape[0]
    order = slot_rows[0]
    resid_list = []
    ctx_list = []
    for micro_idx in range(micro_count):
        partial_value = jnp.dot(context[micro_idx], w_out, preferred_element_type=jnp.float32)
        summed = lax.psum(partial_value.astype(jnp.bfloat16), "tensor").astype(jnp.float32)
        grad_rows = norm_backward(residual[micro_idx], summed, gain, cotangent[micro_idx])
        resid_list.append(grad_rows)
        ctx_back = lax.dot_general(
            grad_rows, w_out, (((1,), (1,)), ((), ())), preferred_element_type=jnp.float32
        )
        ctx_list.append(ctx_back.astype(jnp.bfloat16))
    replicas = lax.axis_size("dp")
    gradient = weight_term(resid_list[0], jnp.take(context[0], order, axis=1))
    micro_idx = 1
    gradient = gradient + weight_term(
        resid_list[micro_idx], jnp.take(context[micro_idx], order, axis=1)
    )
    reduced = lax.psum_scatter(gradient, "dp", scatter_dimension=0, tiled=True)
    grad_slots = (reduced / replicas)[None]
    return (grad_slots, jnp.stack(ctx_list), jnp.stack(resid_list))


def solution(mesh):
    in_specs = (
        P(None, "dp", None),
        P(None, "dp", "tensor"),
        P("tensor", None),
        P(),
        P(None, "dp", None),
        P("tensor", None),
    )
    out_specs = (P("tensor", "dp", None), P(None, "dp", "tensor"), P(None, "dp", None))
    return jax.shard_map(body, mesh=mesh, in_specs=in_specs, out_specs=out_specs, check_vma=False)
```

profile of v0, /device:TPU:0, one launch (start us, length us, event | category | flops | bytes accessed | tf_op | source)
XLA Modules:
  0.0 133.7 jit_solution(9000299881545340281)
XLA Ops:
  7.2 0.0 copy-start.6
  7.2 0.0 all-reduce.3.cloned.1.call-start
  7.2 0.0 copy-start
  7.2 4.0 %convolution_convert_fusion = bf16[64,5120]{1,0:T(8,128)(2,1)} fusion(bf16[384,5120]{1,0:T(8,128)(2,1)} %param.10, bf16[2,64,384]{2,1,0:T(8,128)(2,1)} %param.9), kind=kOutput, calls=%fused_computation.2 | convolution fusion | flops 251985920 | bytes 4636672 | tf_op jit(solution)/shard_map/dot_general | solution.py:33
  11.2 0.0 copy-done.6
  11.2 0.0 copy-done
  11.2 1.7 %convolution_convert_fusion.1 = bf16[64,5120]{1,0:T(8,128)(2,1)} fusion(bf16[384,5120]{1,0:T(8,128)(2,1)S(1)} %copy-done, bf16[2,64,384]{2,1,0:T(8,128)(2,1)S(1)} %copy-done.6), kind=kOutput, calls=%fused_computation.3 | convolution fusion | flops 251985920 | bytes 4636672 | tf_op jit(solution)/shard_map/dot_general | solution.py:33
  12.9 0.0 copy-start.8
  12.9 0.0 copy-start.2
  12.9 0.0 all-reduce.3.cloned.1.call-update
  12.9 0.0 reduce-scatter.2.cloned.1.call-start
  13.0 0.1 copy.12
  13.1 0.1 copy.11
  13.2 0.3 copy-done.8
  13.5 0.6 gather_fusion.1
  14.1 0.6 gather_fusion
  14.7 40.2 %all-reduce.3.cloned.1.call-done = (bf16[64,5120]{1,0:T(8,128)(2,1)}, bf16[64,5120]{1,0:T(8,128)(2,1)}) async-done(((bf16[64,5120]{1,0:T(8,128)(2,1)}, bf16[64,5120]{1,0:T(8,128)(2,1)}), (bf16[64,5120]{1,0:T(8,128)(2,1)}, bf16[64,5120]{1,0:T(8,128)(2,1)})) %all-reduce.3.cloned.1.call-update) | async-done | bytes 1310736 | tf_op jit(solution)/shard_map/psum | solution.py:34
  54.9 0.0 copy-done.2
  54.9 0.0 copy-start.3
  54.9 0.0 copy-start.4
  54.9 1.8 %fusion.17 = (f32[64]{0:T(128)S(1)}, f32[64]{0:T(128)S(1)}) fusion(bf16[64,5120]{1,0:T(8,128)(2,1)} %get-tuple-element.13, bf16[2,64,5120]{2,1,0:T(8,128)(2,1)S(1)} %copy-done.2, bf16[64,5120]{1,0:T(8,128)(2,1)} %get-tuple-element.12), kind=kLoop, calls=%fused_computation.29 | loop fusion | flops 2621312 | bytes 2621952 | tf_op jit(solution)/shard_map/reduce_sum | solution.py:9
  56.8 0.0 copy-done.3
  56.8 0.0 copy-done.4
  56.8 0.0 copy-start.5
  56.8 0.0 copy-start.7
  56.8 0.6 multiply_reduce_fusion
  57.5 0.6 copy-done.5
  58.1 0.0 copy-done.7
  58.1 1.0 fusion.6
  59.2 1.3 fusion.5
  60.5 0.3 fusion.23
  60.8 1.1 convolution_add_fusion
  61.9 0.0 reduce-scatter.2.cloned.1.call-update
  61.9 0.0 copy-start.1
  61.9 3.6 %fusion.19 = bf16[1,64,384]{2,1,0:T(8,128)(2,1)S(1)} fusion(bf16[64,5120]{1,0:T(8,128)(2,1)S(1)} %get-tuple-element.14, bf16[384,5120]{1,0:T(8,128)(2,1)} %param.10), kind=kOutput, calls=%fused_computation.33 | convolution fusion | flops 251682816 | bytes 4636672 | tf_op jit(solution)/shard_map/dot_general | solution.py:37
  65.5 0.0 copy-done.1
  65.5 1.3 fusion.18
  66.9 0.7 pad_maximum_fusion.1
  67.5 1.2 pad_maximum_fusion
  68.7 56.7 %reduce-scatter.2.cloned.1.call-done = f32[640,32]{0,1:T(8,128)} async-done(((f32[5120,32]{0,1:T(8,128)}), f32[640,32]{0,1:T(8,128)}) %reduce-scatter.2.cloned.1.call-update) | async-done | bytes 81936 | tf_op jit(solution)/shard_map/reduce_scatter | solution.py:47
  125.4 1.5 %multiply_bitcast_fusion = f32[1,640,32]{1,2,0:T(8,128)} fusion(f32[640,32]{0,1:T(8,128)} %reduce-scatter.2.cloned.1.call-done), kind=kLoop, calls=%fused_computation.35 | loop fusion | flops 20480 | bytes 163840 | tf_op jit(solution)/shard_map/broadcast_in_dim | solution.py:48
  (11 shorter events, 0.1 us)
Async XLA Ops:
  7.2 4.0 %copy-start.6 = (bf16[2,64,384]{2,1,0:T(8,128)(2,1)S(1)}, bf16[2,64,384]{2,1,0:T(8,128)(2,1)}, u32[]{:S(2)}) copy-start(bf16[2,64,384]{2,1,0:T(8,128)(2,1)} %param.9) | copy-start | bytes 294916
  7.2 47.7 %all-reduce.3.cloned.1.call-start = ((), (), s32[]{:S(2)}) async-start(), calls=%async_computation.2 | async-start | bytes 2621440 | tf_op jit(solution)/shard_map/psum | solution.py:34
  7.2 4.0 %copy-start = (bf16[384,5120]{1,0:T(8,128)(2,1)S(1)}, bf16[384,5120]{1,0:T(8,128)(2,1)}, u32[]{:S(2)}) copy-start(bf16[384,5120]{1,0:T(8,128)(2,1)} %param.10) | copy-start | bytes 11796484
  12.9 0.7 copy-start.8
  12.9 42.0 %copy-start.2 = (bf16[2,64,5120]{2,1,0:T(8,128)(2,1)S(1)}, bf16[2,64,5120]{2,1,0:T(8,128)(2,1)}, u32[]{:S(2)}) copy-start(bf16[2,64,5120]{2,1,0:T(8,128)(2,1)} %param.8) | copy-start | bytes 3932164
  12.9 112.5 %reduce-scatter.2.cloned.1.call-start = ((), (), s32[]{:S(2)}) async-start(), calls=%async_computation.1 | async-start | bytes 737280 | tf_op jit(solution)/shard_map/reduce_scatter | solution.py:47
  54.9 1.8 %copy-start.3 = (bf16[64,5120]{1,0:T(8,128)(2,1)S(1)}, bf16[64,5120]{1,0:T(8,128)(2,1)}, u32[]{:S(2)}) copy-start(bf16[64,5120]{1,0:T(8,128)(2,1)} %get-tuple-element.12) | copy-start | bytes 1966084
  54.9 1.9 %copy-start.4 = (bf16[64,5120]{1,0:T(8,128)(2,1)S(1)}, bf16[64,5120]{1,0:T(8,128)(2,1)}, u32[]{:S(2)}) copy-start(bf16[64,5120]{1,0:T(8,128)(2,1)} %get-tuple-element.13) | copy-start | bytes 1966084
  56.8 1.3 copy-start.5
  56.8 1.3 copy-start.7
  61.9 3.6 %copy-start.1 = (bf16[384,5120]{1,0:T(8,128)(2,1)S(1)}, bf16[384,5120]{1,0:T(8,128)(2,1)}, u32[]{:S(2)}) copy-start(bf16[384,5120]{1,0:T(8,128)(2,1)} %param.10) | copy-start | bytes 11796484
Sparse Core Ops, SparseCore 0:
  13.0 41.8 all-reduce.2
  62.1 63.2 reduce-scatter.1
where the time goes:
time: 134 us
  waiting for transfers between devices  96.9 us (72%)
  between operations  14.2 us (11%)
  matrix products  12 us (9%)
  other arithmetic  8.16 us (6%)
  local copies, waits for them, and re-layouts  2.43 us (2%)
    reduce_scatter x1, waiting for transfers between devices, body(): reduced = lax.psum_scatter(gradient, 'dp', scatter_dimension=0, tiled=True)  56.7 us
    psum x1, waiting for transfers between devices, body(): lax.psum(partial_value.astype(jnp.bfloat16), 'tensor').astype(jnp.float32)  40.2 us
    dot_general x2, matrix products, body(): jnp.dot(context[micro_idx], w_out, preferred_element_type=jnp.float32)  5.64 us
    dot_general x2, matrix products, body(): lax.dot_general(grad_rows, w_out, (((1,), (1,)), ((), ())), preferred_ele...  4.89 us
  transfers between devices with their start and end apart: 2, of which 2 were waited for; matrix products, arithmetic and copies ran while one was open for 6% of the time, Pallas kernels for 0%

commit v1 on v0

v1 whole, which is shorter than its diff:
```python
import functools

import jax
import jax.numpy as jnp
from jax import lax
from jax.experimental import pallas as pl
from jax.experimental.pallas import tpu as pltpu
from jax.sharding import PartitionSpec as P

MESH = pl.DeviceIdType.MESH
ANY = pl.BlockSpec(memory_space=pl.ANY)
VMEM = pl.BlockSpec(memory_space=pltpu.VMEM)
F32 = jnp.float32
BF16 = jnp.bfloat16
LANES = 128
ROWS = 16


def pieces_of(width):
    for count in (4, 2):
        if width % (count * LANES) == 0:
            return count
    return 1


def norm_backward(hidden, cot_rows, gain):
    scale = 1.0 / hidden.shape[-1]
    center = hidden - jnp.sum(hidden, axis=-1, keepdims=True) * scale
    inverse = lax.rsqrt(jnp.sum(center * center, axis=-1, keepdims=True) * scale + 1e-05)
    upstream = cot_rows.astype(F32) * gain
    mean_up = jnp.sum(upstream, axis=-1, keepdims=True) * scale
    slope = jnp.sum(upstream * center, axis=-1, keepdims=True) * scale * inverse * inverse
    return (inverse * (upstream - mean_up - center * slope)).astype(BF16)


def kernel(reduce_dp, replicas, tensors, res_hbm, ctx_hbm, w_hbm, gain_hbm, cot_hbm, slot_ref,
           slots_out, ctx_out, resid_out,
           ctx, w, res, cot, gain, lhs, psend, precv, own, ysum, resid, gsend, grecv, gown,
           load_sem, w_sem, store_sem, p_send, p_recv, y_send, y_recv, r_send, r_recv, g_send, g_recv):
    rows, width = resid.shape
    half = rows // 2
    chips = tensors // 2
    dp = lax.axis_index("dp")
    tensor = lax.axis_index("tensor")
    chip, core = tensor // 2, tensor % 2
    mate = chip * 2 + (1 - core)
    mine = pl.multiple_of(core * half, half)
    theirs = pl.multiple_of((1 - core) * half, half)
    count = pieces_of(width)
    cols = width // count
    chunks = half // ROWS
    bucket = slot_ref.shape[1]

    load_ctx = pltpu.make_async_copy(ctx_hbm, ctx, load_sem.at[0])
    load_ctx.start()
    loads_w = []
    for j in range(count):
        span = pl.ds(j * cols, cols)
        copy = pltpu.make_async_copy(w_hbm.at[:, span], w.at[:, span], w_sem.at[j])
        copy.start()
        loads_w.append(copy)
    load_rest = [
        pltpu.make_async_copy(res_hbm.at[pl.ds(mine, half)], res, load_sem.at[1]),
        pltpu.make_async_copy(cot_hbm.at[pl.ds(mine, half)], cot, load_sem.at[2]),
        pltpu.make_async_copy(gain_hbm, gain, load_sem.at[3]),
    ]
    for copy in load_rest:
        copy.start()

    barrier = pltpu.get_barrier_semaphore()
    pl.semaphore_signal(barrier, inc=1, device_id={"dp": dp, "tensor": mate}, device_id_type=MESH)
    greeted = 1
    for i in range(1, chips):
        other = lax.rem(chip + i, chips) * 2 + core
        pl.semaphore_signal(barrier, inc=1, device_id={"dp": dp, "tensor": other}, device_id_type=MESH)
        greeted += 1
    if reduce_dp:
        for i in range(1, replicas):
            pl.semaphore_signal(barrier, inc=1, device_id={"dp": lax.rem(dp + i, replicas), "tensor": tensor},
                                device_id_type=MESH)
            greeted += 1

    load_ctx.wait()
    lhs[pl.ds(0, half)] = ctx[pl.ds(theirs, half)]
    lhs[pl.ds(half, half)] = ctx[pl.ds(mine, half)]

    def to_mate(j):
        span = pl.ds(j * cols, cols)
        return pltpu.make_async_remote_copy(
            src_ref=psend.at[:, span], dst_ref=precv.at[:, span], send_sem=p_send.at[j], recv_sem=p_recv.at[j],
            device_id={"dp": dp, "tensor": mate}, device_id_type=MESH)

    for j in range(count):
        span = pl.ds(j * cols, cols)
        loads_w[j].wait()
        product = jnp.dot(lhs[...], w[:, span], preferred_element_type=F32)
        psend[:, span] = product[:half].astype(BF16)
        own[:, span] = product[half:]
        if j == 0:
            pl.semaphore_wait(barrier, greeted)
        to_mate(j).start()

    def across(i, piece):
        other = lax.rem(chip + i, chips) * 2 + core
        if piece < count:
            block = ysum.at[chip, pl.ds(0, ROWS), pl.ds(piece * cols, cols)]
        else:
            block = ysum.at[chip, pl.ds((piece - count + 1) * ROWS, ROWS)]
        return pltpu.make_async_remote_copy(
            src_ref=block, dst_ref=block, send_sem=y_send.at[i - 1, piece], recv_sem=y_recv.at[i - 1, piece],
            device_id={"dp": dp, "tensor": other}, device_id_type=MESH)

    total = count + chunks - 1
    for j in range(count):
        span = pl.ds(j * cols, cols)
        to_mate(j).wait_recv()
        ysum[chip, :, span] = (own[:, span] + precv[:, span].astype(F32)).astype(BF16)
        for i in range(1, chips):
            across(i, j).start()
    for piece in range(count, total):
        for i in range(1, chips):
            across(i, piece).start()

    square = (bucket, bucket)
    diagonal = lax.broadcasted_iota(jnp.int32, square, 0) == lax.broadcasted_iota(jnp.int32, square, 1)
    order = jnp.sum(jnp.where(diagonal, slot_ref[...].astype(F32), 0.0), axis=1, keepdims=True)
    place = lax.broadcasted_iota(jnp.int32, (bucket, ctx.shape[1]), 1).astype(F32)
    chosen = jnp.where(place == order, 1.0, 0.0).astype(BF16)
    picked = lax.dot_general(chosen, ctx[...], (((1,), (1,)), ((), ())),
                             preferred_element_type=F32).astype(BF16)

    def share(r):
        span = pl.ds(mine + r * ROWS, ROWS)
        return pltpu.make_async_remote_copy(
            src_ref=resid.at[span], dst_ref=resid.at[span], send_sem=r_send.at[r], recv_sem=r_recv.at[r],
            device_id={"dp": dp, "tensor": mate}, device_id_type=MESH)

    for copy in load_rest:
        copy.wait()
    for r in range(chunks):
        for piece in (range(count) if r == 0 else (count + r - 1,)):
            for i in range(1, chips):
                across(i, piece).wait_recv()
        span = pl.ds(r * ROWS, ROWS)
        summed = ysum[0, span].astype(F32)
        for k in range(1, chips):
            summed = summed + ysum[k, span].astype(F32)
        hidden = res[span].astype(F32) + summed
        resid[pl.ds(pl.multiple_of(mine + r * ROWS, ROWS), ROWS)] = norm_backward(hidden, cot[span], gain[...])
        share(r).start()
    for r in range(chunks):
        share(r).wait_recv()
    store_resid = pltpu.make_async_copy(resid, resid_out, store_sem.at[0])
    store_resid.start()

    def to_peer(i):
        return pltpu.make_async_remote_copy(
            src_ref=gsend.at[i - 1], dst_ref=grecv.at[i - 1], send_sem=g_send.at[i - 1], recv_sem=g_recv.at[i - 1],
            device_id={"dp": lax.rem(dp + i, replicas), "tensor": tensor}, device_id_type=MESH)

    if reduce_dp:
        block = width // replicas
        for i in list(range(1, replicas)) + [0]:
            span = pl.ds(pl.multiple_of(lax.rem(dp + i, replicas) * block, block), block)
            gradient = jnp.dot(picked, resid[:, span], preferred_element_type=F32)
            if i == 0:
                gown[...] = gradient
            else:
                gsend[i - 1] = gradient.astype(BF16)
                to_peer(i).start()
    else:
        for j in range(count):
            span = pl.ds(j * cols, cols)
            slots_out[:, span] = jnp.dot(picked, resid[:, span], preferred_element_type=F32)

    back = None
    for j in range(count):
        span = pl.ds(j * cols, cols)
        term = lax.dot_general(resid[:, span], w[:, span], (((1,), (1,)), ((), ())), preferred_element_type=F32)
        back = term if back is None else back + term
    ctx_out[...] = back.astype(BF16)

    if reduce_dp:
        gradient = gown[...]
        for i in range(1, replicas):
            to_peer(i).wait_recv()
            gradient = gradient + grecv[i - 1].astype(F32)
        slots_out[...] = gradient * (1.0 / replicas)
    for j in range(count):
        to_mate(j).wait_send()
    for piece in range(total):
        for i in range(1, chips):
            across(i, piece).wait_send()
    for r in range(chunks):
        share(r).wait_send()
    if reduce_dp:
        for i in range(1, replicas):
            to_peer(i).wait_send()
    store_resid.wait()


def body(replicas, tensors, residual, context, w_out, gain, cotangent, slot_rows):
    micro, tokens, width = residual.shape
    depth = w_out.shape[0]
    bucket = slot_rows.shape[1]
    rows = micro * tokens
    half = rows // 2
    chips = tensors // 2
    count = pieces_of(width)
    pieces = count + half // ROWS - 1
    reduce_dp = width % (replicas * LANES) == 0
    block = width // replicas if reduce_dp else LANES
    peers = max(replicas - 1, 1) if reduce_dp else 1
    dma = pltpu.SemaphoreType.DMA
    slots, ctx_grad, resid = pl.pallas_call(
        functools.partial(kernel, reduce_dp, replicas, tensors),
        out_shape=(
            jax.ShapeDtypeStruct((bucket, block if reduce_dp else width), F32),
            jax.ShapeDtypeStruct((rows, depth), BF16),
            jax.ShapeDtypeStruct((rows, width), BF16),
        ),
        in_specs=[ANY] * 5 + [VMEM],
        out_specs=(VMEM, VMEM, ANY),
        scratch_shapes=[
            pltpu.VMEM((rows, depth), BF16),
            pltpu.VMEM((depth, width), BF16),
            pltpu.VMEM((half, width), BF16),
            pltpu.VMEM((half, width), BF16),
            pltpu.VMEM((1, width), F32),
            pltpu.VMEM((rows, depth), BF16),
            pltpu.VMEM((half, width), BF16),
            pltpu.VMEM((half, width), BF16),
            pltpu.VMEM((half, width), F32),
            pltpu.VMEM((chips, half, width), BF16),
            pltpu.VMEM((rows, width), BF16),
            pltpu.VMEM((peers, bucket, block), BF16),
            pltpu.VMEM((peers, bucket, block), BF16),
            pltpu.VMEM((bucket, block), F32),
            dma((4,)), dma((count,)), dma((1,)), dma((count,)), dma((count,)),
            dma((max(chips - 1, 1), pieces)), dma((max(chips - 1, 1), pieces)),
            dma((half // ROWS,)), dma((half // ROWS,)), dma((peers,)), dma((peers,)),
        ],
        compiler_params=pltpu.CompilerParams(
            collective_id=0, has_side_effects=True, vmem_limit_bytes=60 * 1024 * 1024),
    )(residual.reshape(rows, width), context.reshape(rows, depth), w_out, gain.reshape(1, width),
      cotangent.reshape(rows, width), slot_rows)
    if not reduce_dp:
        slots = lax.psum_scatter(slots, "dp", scatter_dimension=1, tiled=True) / replicas
    return (slots.T[None], ctx_grad.reshape(micro, tokens, depth), resid.reshape(micro, tokens, width))


def solution(mesh):
    in_specs = (
        P(None, "dp", None),
        P(None, "dp", "tensor"),
        P("tensor", None),
        P(),
        P(None, "dp", None),
        P("tensor", None),
    )
    out_specs = (P("tensor", "dp", None), P(None, "dp", "tensor"), P(None, "dp", None))
    step = functools.partial(body, mesh.shape["dp"], mesh.shape["tensor"])
    return jax.shard_map(step, mesh=mesh, in_specs=in_specs, out_specs=out_specs, check_vma=False)
```

time: 134 us -> 40.2 us (0.30)
  waiting for transfers between devices: 96.9 us -> 0 us
  Pallas kernels: 0 us -> 33.4 us
  between operations: 14.2 us -> 0.64 us
  matrix products: 12 us -> 0 us
  other arithmetic: 8.16 us -> 0 us
  local copies, waits for them, and re-layouts: 2.43 us -> 5.53 us
    reduce_scatter x1 -> x0, waiting for transfers between devices: 56.7 us -> none  [body(): reduced = lax.psum_scatter(gradient, 'dp', scatter_dimension=0, tiled=True)]
    psum x1 -> x0, waiting for transfers between devices: 40.2 us -> none  [body(): lax.psum(partial_value.astype(jnp.bfloat16), 'tensor').astype(jnp.float32)]
    pallas_call x0 -> x1, Pallas kernels: none -> 33.4 us  [body(): pl.pallas_call(functools.partial(kernel, reduce_dp, replicas, tensors), o...]
    dot_general x6 -> x0, matrix products: 12 us -> none  [the longest x2 5.64 us: body(): jnp.dot(context[micro_idx], w_out, preferred_element_type=jnp.float32)]
    unnamed x20 -> x3, local copies, waits for them, and re-layouts: 1.24 us -> 5.53 us
    reduce_sum x3 -> x0, other arithmetic: 3.5 us -> none  [the longest x1 1.82 us: norm_backward(): center = hidden - jnp.mean(hidden, axis=-1, keepdims=True)]
    another operation x2 -> x0, other arithmetic: 1.83 us -> none  [body(): return (grad_slots, jnp.stack(ctx_list), jnp.stack(resid_list))]
    broadcast_in_dim x1 -> x0, other arithmetic: 1.53 us -> none  [body(): grad_slots = (reduced / replicas)[None]]
  transfers between devices with their start and end apart: 2 -> 0, of which waited for: 2 -> 0; matrix products, arithmetic and copies ran while one was open for 6% -> 0% of each run, Pallas kernels for 0% -> 0%
where the time goes in v1:
time: 40.2 us; the launch traced here: 39.6 us
  Pallas kernels  33.4 us (83%)
  local copies, waits for them, and re-layouts  5.53 us (14%)
  between operations  0.64 us (2%)
    pallas_call x1, Pallas kernels, body(): pl.pallas_call(functools.partial(kernel, reduce_dp, replicas, tensors), o...  33.4 us
    unnamed x3, local copies, waits for them, and re-layouts  5.53 us

profile of v1, /device:TPU:0, one launch (start us, length us, event | category | flops | bytes accessed | tf_op | source)
XLA Modules:
  0.0 39.6 jit_solution(3083748253457249658)
XLA Ops:
  0.6 33.4 %shard_map.85 = (f32[32,640]{1,0:T(8,128)}, bf16[128,384]{1,0:T(8,128)(2,1)}, bf16[128,5120]{1,0:T(8,128)(2,1)}) custom-call(bf16[128,5120]{1,0:T(8,128)(2,1)} %bitcast.10, bf16[128,384]{1,0:T(8,128)(2,1)} %bitcast.13, bf16[384,5120]{1,0:T(8,128)(2,1)} %w_hbm.1, f32[1,5120]{1,0:T(1,128)} %bitcast.15, bf16[128,5120]{1,0:T(8,128)(2,1)} %bitcast.11, ...), custom_call_target="tpu_custom_call" | custom-call | tf_op jit(solution)/shard_map/pallas_call | solution.py:215
  34.1 1.5 %copy.12 = f32[1,640,32]{1,2,0:T(8,128)} copy(f32[1,640,32]{1,2,0:T(8,128)} %bitcast.14) | data formatting | bytes 163840
  35.6 1.5 %copy.13 = bf16[2,64,384]{2,1,0:T(8,128)(2,1)} copy(bf16[2,64,384]{2,1,0:T(8,128)(2,1)} %bitcast.12) | data formatting | bytes 196608
  37.1 2.5 %copy.14 = bf16[2,64,5120]{2,1,0:T(8,128)(2,1)} copy(bf16[2,64,5120]{2,1,0:T(8,128)(2,1)} %bitcast.9) | data formatting | bytes 2621440

commit v2 on v1

--- a/solution.py
+++ b/solution.py
@@ -14,6 +14,7 @@
 BF16 = jnp.bfloat16
 LANES = 128
 ROWS = 16
+VMEM_BYTES = 67043328
 
 
 def pieces_of(width):
@@ -34,9 +35,9 @@
 
 
 def kernel(reduce_dp, replicas, tensors, res_hbm, ctx_hbm, w_hbm, gain_hbm, cot_hbm, slot_ref,
-           slots_out, ctx_out, resid_out,
-           ctx, w, res, cot, gain, lhs, psend, precv, own, ysum, resid, gsend, grecv, gown,
-           load_sem, w_sem, store_sem, p_send, p_recv, y_send, y_recv, r_send, r_recv, g_send, g_recv):
+           slots_out, ctx_out, resid,
+           ctx, w, res, cot, gain, lhs, psend, precv, own, ysum, gsend, grecv, gown,
+           load_sem, w_sem, p_send, p_recv, y_send, y_recv, r_send, r_recv, g_send, g_recv):
     rows, width = resid.shape
     half = rows // 2
     chips = tensors // 2
@@ -150,8 +151,6 @@
         share(r).start()
     for r in range(chunks):
         share(r).wait_recv()
-    store_resid = pltpu.make_async_copy(resid, resid_out, store_sem.at[0])
-    store_resid.start()
 
     def to_peer(i):
         return pltpu.make_async_remote_copy(
@@ -196,7 +195,26 @@
     if reduce_dp:
         for i in range(1, replicas):
             to_peer(i).wait_send()
-    store_resid.wait()
+
+
+def store_kernel(count, *refs):
+    copies = [pltpu.make_async_copy(refs[i], refs[count + i], refs[2 * count].at[i]) for i in range(count)]
+    for copy in copies:
+        copy.start()
+    for copy in copies:
+        copy.wait()
+
+
+def store(*arrays):
+    count = len(arrays)
+    return pl.pallas_call(
+        functools.partial(store_kernel, count),
+        out_shape=tuple(jax.ShapeDtypeStruct(a.shape, a.dtype) for a in arrays),
+        in_specs=[ANY] * count,
+        out_specs=(ANY,) * count,
+        scratch_shapes=[pltpu.SemaphoreType.DMA((count,))],
+        compiler_params=pltpu.CompilerParams(vmem_limit_bytes=1024 * 1024),
+    )(*arrays)
 
 
 def body(replicas, tensors, residual, context, w_out, gain, cotangent, slot_rows):
@@ -212,15 +230,16 @@
     block = width // replicas if reduce_dp else LANES
     peers = max(replicas - 1, 1) if reduce_dp else 1
     dma = pltpu.SemaphoreType.DMA
+    spare = 4 * bucket * (block if reduce_dp else width) + 2 * rows * (depth + width)
     slots, ctx_grad, resid = pl.pallas_call(
         functools.partial(kernel, reduce_dp, replicas, tensors),
         out_shape=(
-            jax.ShapeDtypeStruct((bucket, block if reduce_dp else width), F32),
-            jax.ShapeDtypeStruct((rows, depth), BF16),
-            jax.ShapeDtypeStruct((rows, width), BF16),
+            pltpu.VMEM((bucket, block if reduce_dp else width), F32),
+            pltpu.VMEM((rows, depth), BF16),
+            pltpu.VMEM((rows, width), BF16),
         ),
         in_specs=[ANY] * 5 + [VMEM],
-        out_specs=(VMEM, VMEM, ANY),
+        out_specs=(VMEM, VMEM, VMEM),
         scratch_shapes=[
             pltpu.VMEM((rows, depth), BF16),
             pltpu.VMEM((depth, width), BF16),
@@ -232,18 +251,18 @@
             pltpu.VMEM((half, width), BF16),
             pltpu.VMEM((half, width), F32),
             pltpu.VMEM((chips, half, width), BF16),
-            pltpu.VMEM((rows, width), BF16),
             pltpu.VMEM((peers, bucket, block), BF16),
             pltpu.VMEM((peers, bucket, block), BF16),
             pltpu.VMEM((bucket, block), F32),
-            dma((4,)), dma((count,)), dma((1,)), dma((count,)), dma((count,)),
+            dma((4,)), dma((count,)), dma((count,)), dma((count,)),
             dma((max(chips - 1, 1), pieces)), dma((max(chips - 1, 1), pieces)),
             dma((half // ROWS,)), dma((half // ROWS,)), dma((peers,)), dma((peers,)),
         ],
         compiler_params=pltpu.CompilerParams(
-            collective_id=0, has_side_effects=True, vmem_limit_bytes=60 * 1024 * 1024),
+            collective_id=0, has_side_effects=True, vmem_limit_bytes=VMEM_BYTES - spare),
     )(residual.reshape(rows, width), context.reshape(rows, depth), w_out, gain.reshape(1, width),
       cotangent.reshape(rows, width), slot_rows)
+    slots, ctx_grad, resid = store(slots, ctx_grad, resid)
     if not reduce_dp:
         slots = lax.psum_scatter(slots, "dp", scatter_dimension=1, tiled=True) / replicas
     return (slots.T[None], ctx_grad.reshape(micro, tokens, depth), resid.reshape(micro, tokens, width))

time: 40.2 us -> 35.1 us (0.87)
  local copies, waits for them, and re-layouts: 5.53 us -> 0 us
  Pallas kernels: 33.4 us -> 33.9 us
    unnamed x3 -> x0, local copies, waits for them, and re-layouts: 5.53 us -> none
    pallas_call x0 -> x1, Pallas kernels: none -> 1.14 us  [store(): pl.pallas_call(functools.partial(store_kernel, count), out_shape=tuple((j...]
    pallas_call x1, Pallas kernels: 33.4 us -> 32.7 us  [body(): pl.pallas_call(functools.partial(kernel, reduce_dp, replicas, tensors), o...]
where the time goes in v2:
time: 35.1 us; the launch traced here: 34.5 us
  Pallas kernels  33.9 us (97%)
  between operations  0.64 us (2%)
    pallas_call x1, Pallas kernels, body(): pl.pallas_call(functools.partial(kernel, reduce_dp, replicas, tensors), o...  32.7 us
    pallas_call x1, Pallas kernels, store(): pl.pallas_call(functools.partial(store_kernel, count), out_shape=tuple((j...  1.14 us

profile of v2, /device:TPU:0, one launch (start us, length us, event | category | flops | bytes accessed | tf_op | source)
XLA Modules:
  0.0 34.5 jit_solution(3141643967033344801)
XLA Ops:
  0.6 32.7 %shard_map.85 = (f32[32,640]{1,0:T(8,128)S(1)}, bf16[128,384]{1,0:T(8,128)(2,1)S(1)}, bf16[128,5120]{1,0:T(8,128)(2,1)S(1)}) custom-call(bf16[128,5120]{1,0:T(8,128)(2,1)} %bitcast.9, bf16[128,384]{1,0:T(8,128)(2,1)} %bitcast.11, bf16[384,5120]{1,0:T(8,128)(2,1)} %w_hbm.1, f32[1,5120]{1,0:T(1,128)} %bitcast.12, bf16[128,5120]{1,0:T(8,128)(2,1)} %bitcast.10, ...), custom_call_target="tpu_custom_call" | custom-call | tf_op jit(solution)/shard_map/pallas_call | solution.py:234
  33.4 1.1 %shard_map.86 = (f32[32,640]{1,0:T(8,128)}, bf16[128,384]{1,0:T(8,128)(2,1)}, bf16[128,5120]{1,0:T(8,128)(2,1)}) custom-call(f32[32,640]{1,0:T(8,128)S(1)} %get-tuple-element.9.refs_0_, bf16[128,384]{1,0:T(8,128)(2,1)S(1)} %get-tuple-element.10.refs_1_, bf16[128,5120]{1,0:T(8,128)(2,1)S(1)} %get-tuple-element.11.refs_2_), custom_call_target="tpu_custom_call" | custom-call | tf_op jit(solution)/shard_map/pallas_call | solution.py:210

commit v3 on v2

--- a/solution.py
+++ b/solution.py
@@ -18,7 +18,7 @@
 
 
 def pieces_of(width):
-    for count in (4, 2):
+    for count in (8, 4, 2):
         if width % (count * LANES) == 0:
             return count
     return 1
@@ -37,7 +37,7 @@
 def kernel(reduce_dp, replicas, tensors, res_hbm, ctx_hbm, w_hbm, gain_hbm, cot_hbm, slot_ref,
            slots_out, ctx_out, resid,
            ctx, w, res, cot, gain, lhs, psend, precv, own, ysum, gsend, grecv, gown,
-           load_sem, w_sem, p_send, p_recv, y_send, y_recv, r_send, r_recv, g_send, g_recv):
+           load_sem, w_sem, p_send, p_recv, y_send, y_recv, r_send, r_recv, g_send, g_recv, ladder):
     rows, width = resid.shape
     half = rows // 2
     chips = tensors // 2
@@ -75,11 +75,26 @@
         other = lax.rem(chip + i, chips) * 2 + core
         pl.semaphore_signal(barrier, inc=1, device_id={"dp": dp, "tensor": other}, device_id_type=MESH)
         greeted += 1
+
+    lower, upper = dp >= 2, dp + 2 < replicas
+    degree = 1 + lower.astype(jnp.int32) + upper.astype(jnp.int32)
+
+    def greet(semaphore):
+        pl.semaphore_signal(semaphore, inc=1, device_id={"dp": dp + 1 - 2 * lax.rem(dp, 2), "tensor": tensor},
+                            device_id_type=MESH)
+
+        @pl.when(lower)
+        def _():
+            pl.semaphore_signal(semaphore, inc=1, device_id={"dp": dp - 2, "tensor": tensor}, device_id_type=MESH)
+
+        @pl.when(upper)
+        def _():
+            pl.semaphore_signal(semaphore, inc=1, device_id={"dp": dp + 2, "tensor": tensor}, device_id_type=MESH)
+
+    rounds = replicas // 2 - 1 if reduce_dp else 0
     if reduce_dp:
-        for i in range(1, replicas):
-            pl.semaphore_signal(barrier, inc=1, device_id={"dp": lax.rem(dp + i, replicas), "tensor": tensor},
-                                device_id_type=MESH)
-            greeted += 1
+        greet(barrier)
+        greeted += degree
 
     load_ctx.wait()
     lhs[pl.ds(0, half)] = ctx[pl.ds(theirs, half)]
@@ -99,6 +114,8 @@
         own[:, span] = product[half:]
         if j == 0:
             pl.semaphore_wait(barrier, greeted)
+            if rounds:
+                greet(ladder.at[0])
         to_mate(j).start()
 
     def across(i, piece):
@@ -149,6 +166,10 @@
         hidden = res[span].astype(F32) + summed
         resid[pl.ds(pl.multiple_of(mine + r * ROWS, ROWS), ROWS)] = norm_backward(hidden, cot[span], gain[...])
         share(r).start()
+        for turn in range(r, rounds, chunks):
+            pl.semaphore_wait(ladder.at[turn], degree)
+            if turn + 1 < rounds:
+                greet(ladder.at[turn + 1])
     for r in range(chunks):
         share(r).wait_recv()
 
@@ -159,7 +180,7 @@
 
     if reduce_dp:
         block = width // replicas
-        for i in list(range(1, replicas)) + [0]:
+        for i in sorted(range(replicas), key=lambda i: -min(i, replicas - i)):
             span = pl.ds(pl.multiple_of(lax.rem(dp + i, replicas) * block, block), block)
             gradient = jnp.dot(picked, resid[:, span], preferred_element_type=F32)
             if i == 0:
@@ -226,7 +247,7 @@
     chips = tensors // 2
     count = pieces_of(width)
     pieces = count + half // ROWS - 1
-    reduce_dp = width % (replicas * LANES) == 0
+    reduce_dp = replicas % 2 == 0 and width % (replicas * LANES) == 0
     block = width // replicas if reduce_dp else LANES
     peers = max(replicas - 1, 1) if reduce_dp else 1
     dma = pltpu.SemaphoreType.DMA
@@ -257,6 +278,7 @@
             dma((4,)), dma((count,)), dma((count,)), dma((count,)),
             dma((max(chips - 1, 1), pieces)), dma((max(chips - 1, 1), pieces)),
             dma((half // ROWS,)), dma((half // ROWS,)), dma((peers,)), dma((peers,)),
+            pltpu.SemaphoreType.REGULAR((max(replicas // 2 - 1, 1) if reduce_dp else 1,)),
         ],
         compiler_params=pltpu.CompilerParams(
             collective_id=0, has_side_effects=True, vmem_limit_bytes=VMEM_BYTES - spare),

time: 35.1 us -> 36.3 us (1.034); the launches traced: 34.5 us -> 36.1 us
  Pallas kernels: 33.9 us -> 35.5 us
    pallas_call x1, Pallas kernels: 32.7 us -> 34.3 us  [body(): pl.pallas_call(functools.partial(kernel, reduce_dp, replicas, tensors), o...]
where the time goes in v3:
time: 36.3 us; the launch traced here: 36.1 us
  Pallas kernels  35.5 us (98%)
  between operations  0.64 us (2%)
    pallas_call x1, Pallas kernels, body(): pl.pallas_call(functools.partial(kernel, reduce_dp, replicas, tensors), o...  34.3 us
    pallas_call x1, Pallas kernels, store(): pl.pallas_call(functools.partial(store_kernel, count), out_shape=tuple((j...  1.14 us

profile of v3, /device:TPU:0, one launch (start us, length us, event | category | flops | bytes accessed | tf_op | source)
XLA Modules:
  0.0 36.1 jit_solution(16636350985589267773)
XLA Ops:
  0.6 34.3 %shard_map.85 = (f32[32,640]{1,0:T(8,128)S(1)}, bf16[128,384]{1,0:T(8,128)(2,1)S(1)}, bf16[128,5120]{1,0:T(8,128)(2,1)S(1)}) custom-call(bf16[128,5120]{1,0:T(8,128)(2,1)} %bitcast.9, bf16[128,384]{1,0:T(8,128)(2,1)} %bitcast.11, bf16[384,5120]{1,0:T(8,128)(2,1)} %w_hbm.1, f32[1,5120]{1,0:T(1,128)} %bitcast.12, bf16[128,5120]{1,0:T(8,128)(2,1)} %bitcast.10, ...), custom_call_target="tpu_custom_call" | custom-call | tf_op jit(solution)/shard_map/pallas_call | solution.py:255
  35.0 1.1 %shard_map.86 = (f32[32,640]{1,0:T(8,128)}, bf16[128,384]{1,0:T(8,128)(2,1)}, bf16[128,5120]{1,0:T(8,128)(2,1)}) custom-call(f32[32,640]{1,0:T(8,128)S(1)} %get-tuple-element.9.refs_0_, bf16[128,384]{1,0:T(8,128)(2,1)S(1)} %get-tuple-element.10.refs_1_, bf16[128,5120]{1,0:T(8,128)(2,1)S(1)} %get-tuple-element.11.refs_2_), custom_call_target="tpu_custom_call" | custom-call | tf_op jit(solution)/shard_map/pallas_call | solution.py:231

commit v4 on v3

--- a/solution.py
+++ b/solution.py
@@ -18,7 +18,7 @@
 
 
 def pieces_of(width):
-    for count in (8, 4, 2):
+    for count in (4, 2):
         if width % (count * LANES) == 0:
             return count
     return 1
@@ -34,9 +34,9 @@
     return (inverse * (upstream - mean_up - center * slope)).astype(BF16)
 
 
-def kernel(reduce_dp, replicas, tensors, res_hbm, ctx_hbm, w_hbm, gain_hbm, cot_hbm, slot_ref,
+def kernel(reduce_dp, replicas, tensors, res_hbm, ctx_hbm, w_hbm, gain_hbm, cot_hbm, slot_hbm,
            slots_out, ctx_out, resid,
-           ctx, w, res, cot, gain, lhs, psend, precv, own, ysum, gsend, grecv, gown,
+           ctx, w, res, cot, gain, slot_ref, lhs, psend, precv, own, ysum, gsend, grecv, gown,
            load_sem, w_sem, p_send, p_recv, y_send, y_recv, r_send, r_recv, g_send, g_recv, ladder):
     rows, width = resid.shape
     half = rows // 2
@@ -64,6 +64,7 @@
         pltpu.make_async_copy(res_hbm.at[pl.ds(mine, half)], res, load_sem.at[1]),
         pltpu.make_async_copy(cot_hbm.at[pl.ds(mine, half)], cot, load_sem.at[2]),
         pltpu.make_async_copy(gain_hbm, gain, load_sem.at[3]),
+        pltpu.make_async_copy(slot_hbm, slot_ref, load_sem.at[4]),
     ]
     for copy in load_rest:
         copy.start()
@@ -139,6 +140,8 @@
         for i in range(1, chips):
             across(i, piece).start()
 
+    for copy in load_rest:
+        copy.wait()
     square = (bucket, bucket)
     diagonal = lax.broadcasted_iota(jnp.int32, square, 0) == lax.broadcasted_iota(jnp.int32, square, 1)
     order = jnp.sum(jnp.where(diagonal, slot_ref[...].astype(F32), 0.0), axis=1, keepdims=True)
@@ -153,8 +156,6 @@
             src_ref=resid.at[span], dst_ref=resid.at[span], send_sem=r_send.at[r], recv_sem=r_recv.at[r],
             device_id={"dp": dp, "tensor": mate}, device_id_type=MESH)
 
-    for copy in load_rest:
-        copy.wait()
     for r in range(chunks):
         for piece in (range(count) if r == 0 else (count + r - 1,)):
             for i in range(1, chips):
@@ -180,7 +181,7 @@
 
     if reduce_dp:
         block = width // replicas
-        for i in sorted(range(replicas), key=lambda i: -min(i, replicas - i)):
+        for i in list(range(1, replicas)) + [0]:
             span = pl.ds(pl.multiple_of(lax.rem(dp + i, replicas) * block, block), block)
             gradient = jnp.dot(picked, resid[:, span], preferred_element_type=F32)
             if i == 0:
@@ -259,7 +260,7 @@
             pltpu.VMEM((rows, depth), BF16),
             pltpu.VMEM((rows, width), BF16),
         ),
-        in_specs=[ANY] * 5 + [VMEM],
+        in_specs=[ANY] * 6,
         out_specs=(VMEM, VMEM, VMEM),
         scratch_shapes=[
             pltpu.VMEM((rows, depth), BF16),
@@ -267,6 +268,7 @@
             pltpu.VMEM((half, width), BF16),
             pltpu.VMEM((half, width), BF16),
             pltpu.VMEM((1, width), F32),
+            pltpu.VMEM((1, bucket), jnp.int32),
             pltpu.VMEM((rows, depth), BF16),
             pltpu.VMEM((half, width), BF16),
             pltpu.VMEM((half, width), BF16),
@@ -275,7 +277,7 @@
             pltpu.VMEM((peers, bucket, block), BF16),
             pltpu.VMEM((peers, bucket, block), BF16),
             pltpu.VMEM((bucket, block), F32),
-            dma((4,)), dma((count,)), dma((count,)), dma((count,)),
+            dma((5,)), dma((count,)), dma((count,)), dma((count,)),
             dma((max(chips - 1, 1), pieces)), dma((max(chips - 1, 1), pieces)),
             dma((half // ROWS,)), dma((half // ROWS,)), dma((peers,)), dma((peers,)),
             pltpu.SemaphoreType.REGULAR((max(replicas // 2 - 1, 1) if reduce_dp else 1,)),

time: 36.3 us -> 33.8 us (0.931)
  the two profiles are of different devices: /device:TPU:0 before, /device:TPU:1 now
where the time goes in v4:
time: 33.8 us; the launch traced here: 33.7 us
  Pallas kernels  33 us (98%)
  between operations  0.64 us (2%)
    pallas_call x1, Pallas kernels, body(): pl.pallas_call(functools.partial(kernel, reduce_dp, replicas, tensors), o...  31.9 us
    pallas_call x1, Pallas kernels, store(): pl.pallas_call(functools.partial(store_kernel, count), out_shape=tuple((j...  1.14 us

profile of v4, /device:TPU:1, one launch (start us, length us, event | category | flops | bytes accessed | tf_op | source)
XLA Modules:
  0.0 33.7 jit_solution(182279584111236651)
XLA Ops:
  0.6 31.9 %shard_map.85 = (f32[32,640]{1,0:T(8,128)S(1)}, bf16[128,384]{1,0:T(8,128)(2,1)S(1)}, bf16[128,5120]{1,0:T(8,128)(2,1)S(1)}) custom-call(bf16[128,5120]{1,0:T(8,128)(2,1)} %bitcast.9, bf16[128,384]{1,0:T(8,128)(2,1)} %bitcast.11, bf16[384,5120]{1,0:T(8,128)(2,1)} %w_hbm.1, f32[1,5120]{1,0:T(1,128)} %bitcast.12, bf16[128,5120]{1,0:T(8,128)(2,1)} %bitcast.10, ...), custom_call_target="tpu_custom_call" | custom-call | tf_op jit(solution)/shard_map/pallas_call | solution.py:256
  32.5 1.1 %shard_map.86 = (f32[32,640]{1,0:T(8,128)}, bf16[128,384]{1,0:T(8,128)(2,1)}, bf16[128,5120]{1,0:T(8,128)(2,1)}) custom-call(f32[32,640]{1,0:T(8,128)S(1)} %get-tuple-element.9.refs_0_, bf16[128,384]{1,0:T(8,128)(2,1)S(1)} %get-tuple-element.10.refs_1_, bf16[128,5120]{1,0:T(8,128)(2,1)S(1)} %get-tuple-element.11.refs_2_), custom_call_target="tpu_custom_call" | custom-call | tf_op jit(solution)/shard_map/pallas_call | solution.py:232

commit v5 on v4

--- a/solution.py
+++ b/solution.py
@@ -18,7 +18,7 @@
 
 
 def pieces_of(width):
-    for count in (4, 2):
+    for count in (5, 4, 2):
         if width % (count * LANES) == 0:
             return count
     return 1
@@ -115,9 +115,9 @@
         own[:, span] = product[half:]
         if j == 0:
             pl.semaphore_wait(barrier, greeted)
-            if rounds:
-                greet(ladder.at[0])
         to_mate(j).start()
+        if j == 0 and rounds:
+            greet(ladder.at[0])
 
     def across(i, piece):
         other = lax.rem(chip + i, chips) * 2 + core
@@ -167,7 +167,7 @@
         hidden = res[span].astype(F32) + summed
         resid[pl.ds(pl.multiple_of(mine + r * ROWS, ROWS), ROWS)] = norm_backward(hidden, cot[span], gain[...])
         share(r).start()
-        for turn in range(r, rounds, chunks):
+        for turn in range(r * rounds // chunks, (r + 1) * rounds // chunks):
             pl.semaphore_wait(ladder.at[turn], degree)
             if turn + 1 < rounds:
                 greet(ladder.at[turn + 1])

time: 33.8 us -> 33.8 us (level)
  the two profiles are of different devices: /device:TPU:1 before, /device:TPU:0 now
where the time goes in v5:
time: 33.8 us; the launch traced here: 33.2 us
  Pallas kernels  32.6 us (96%)
  between operations  0.64 us (2%)
    pallas_call x1, Pallas kernels, body(): pl.pallas_call(functools.partial(kernel, reduce_dp, replicas, tensors), o...  31.4 us
    pallas_call x1, Pallas kernels, store(): pl.pallas_call(functools.partial(store_kernel, count), out_shape=tuple((j...  1.14 us

profile of v5, /device:TPU:0, one launch (start us, length us, event | category | flops | bytes accessed | tf_op | source)
XLA Modules:
  0.0 33.2 jit_solution(11462273057442973605)
XLA Ops:
  0.6 31.4 %shard_map.85 = (f32[32,640]{1,0:T(8,128)S(1)}, bf16[128,384]{1,0:T(8,128)(2,1)S(1)}, bf16[128,5120]{1,0:T(8,128)(2,1)S(1)}) custom-call(bf16[128,5120]{1,0:T(8,128)(2,1)} %bitcast.9, bf16[128,384]{1,0:T(8,128)(2,1)} %bitcast.11, bf16[384,5120]{1,0:T(8,128)(2,1)} %w_hbm.1, f32[1,5120]{1,0:T(1,128)} %bitcast.12, bf16[128,5120]{1,0:T(8,128)(2,1)} %bitcast.10, ...), custom_call_target="tpu_custom_call" | custom-call | tf_op jit(solution)/shard_map/pallas_call | solution.py:256
  32.1 1.1 %shard_map.86 = (f32[32,640]{1,0:T(8,128)}, bf16[128,384]{1,0:T(8,128)(2,1)}, bf16[128,5120]{1,0:T(8,128)(2,1)}) custom-call(f32[32,640]{1,0:T(8,128)S(1)} %get-tuple-element.9.refs_0_, bf16[128,384]{1,0:T(8,128)(2,1)S(1)} %get-tuple-element.10.refs_1_, bf16[128,5120]{1,0:T(8,128)(2,1)S(1)} %get-tuple-element.11.refs_2_), custom_call_target="tpu_custom_call" | custom-call | tf_op jit(solution)/shard_map/pallas_call | solution.py:232
